TPU v7x, 32 devices: a whole 2x2x4 slice. The times are simulated.
32 devices in a mesh: rows: 8 (over y, x, core), cols: 4 (over z).
Axes of the slice: x: 2, y: 2, z: 4, core: 2. Of those that a mesh axis runs over, the one named last changes fastest.
Arguments:
- intensity: float32 [4096, 4096], P('rows', 'cols'), may hold values from -0.5 to 1.5, as said below
- edge_weight: float32 [4096, 4096], P('rows', 'cols'), may hold values from 0.2 to 2
- labels: int32 [4096, 4096], P('rows', 'cols'), may hold values from 0 to 1
- tile_cost: int32 [16, 16], replicated, may hold values from 0 to 3, as said below
- tile_owner: int32 [16, 16], replicated, may hold values from -1 to 31, as said below
Outputs:
- slot_field: float32 [32, 4, 256, 256], P('rows', 'cols')
Inputs may be any that keep to these rules, and one draw needn't show every extreme that they name: `intensity`: intensity of stained tissue. `tile_cost`: 0 marks a background tile, 1 to 3 a tissue tile. `tile_owner`: -1 exactly for background tiles. A tissue tile's value is k * 4 + s: it goes to slot s of the device with rows index k in its own column band; within one band no two tiles share a value; the tiles of one device's block send at most 1 tile to any one device, and in every draw some block sends exactly 1 to one device and some device receives all 4 of its slots filled.
All inputs are finite; a program needn't handle non-finite values.
Results may differ from a plain program's by a relative error of at most 0.0001.
Values sent between devices are 32-bit elements; how exact they have to be, the bound alone decides.
A program may use at most 128 MiB of HBM per device.

v0:
```python
import functools

import jax
import jax.numpy as jnp
from jax import lax
from jax.experimental import pallas as pl
from jax.experimental.pallas import tpu as pltpu
from jax.sharding import PartitionSpec as P

TILE = 256
ITERS_BEFORE = 2
ITERS_AFTER = 2
ITERS = ITERS_BEFORE + ITERS_AFTER

sigma_step = 0.35
tau_step = 0.35
fidelity = 1.0

SUB = 8
LANES = 128
BATCH = 4
TOP = 2 * SUB


def kernel(
    n_rows,
    n_cols,
    cost_ref,
    owner_ref,
    i_hbm,
    e_hbm,
    l_hbm,
    out_ref,
    img,
    edge,
    lab,
    u,
    v,
    p1,
    p2,
    moved,
    wmap,
    colmask,
    rowmask,
    strip_out,
    strip_in,
    part_a,
    got_a,
    part_b,
    got_b,
    tiles,
    pack,
    recv,
    load_sem,
    strip_send,
    strip_recv,
    rim_send,
    rim_recv,
    a_send,
    a_recv,
    b_send,
    b_recv,
    t_send,
    t_recv,
):
    height, width = lab.shape
    wide = img.shape[1]
    tiles_down, tiles_across = height // TILE, width // TILE
    slots = out_ref.shape[0]
    r = lax.axis_index("rows")
    c = lax.axis_index("cols")
    own = pl.ds(TOP, height)
    chunks = height // SUB
    f32 = jnp.float32

    def local(src, dst, k):
        return pltpu.make_async_copy(src, dst, load_sem.at[k])

    loads = [
        local(l_hbm, lab, 0),
        local(i_hbm, img.at[own, pl.ds(0, width)], 1),
        local(e_hbm, edge.at[own, pl.ds(0, width)], 2),
    ]
    for load in loads:
        load.start()

    def row_peer(d):
        return (lax.rem(r + d, n_rows), c)

    def col_peer(d):
        return (r, lax.rem(c + d, n_cols))

    barrier = pltpu.get_barrier_semaphore()
    for d in range(1, n_rows):
        pl.semaphore_signal(barrier, inc=1, device_id=row_peer(d), device_id_type=pl.DeviceIdType.MESH)
    for d in range(1, n_cols):
        pl.semaphore_signal(barrier, inc=1, device_id=col_peer(d), device_id_type=pl.DeviceIdType.MESH)

    def remote(src, dst, send, got, peer):
        return pltpu.make_async_remote_copy(
            src_ref=src, dst_ref=dst, send_sem=send, recv_sem=got,
            device_id=peer, device_id_type=pl.DeviceIdType.MESH,
        )

    lane = lax.broadcasted_iota(jnp.int32, (SUB, LANES), 1)
    sublane = lax.broadcasted_iota(jnp.int32, (SUB, LANES), 0)
    total_bands = n_rows * tiles_down
    total_across = n_cols * tiles_across
    for band in range(tiles_down + 2):
        tr = jnp.clip(r * tiles_down + band - 1, 0, total_bands - 1)
        for t in range(tiles_across):
            w = cost_ref[tr, c * tiles_across + t].astype(f32)
            for h in range(TILE // LANES):
                wmap[band * SUB:(band + 1) * SUB, t * TILE + h * LANES:t * TILE + (h + 1) * LANES] = (
                    jnp.full((SUB, LANES), w * (tau_step * fidelity), f32)
                )
        right = cost_ref[tr, jnp.clip((c + 1) * tiles_across, 0, total_across - 1)].astype(f32)
        left = cost_ref[tr, jnp.clip(c * tiles_across - 1, 0, total_across - 1)].astype(f32)
        wmap[band * SUB:(band + 1) * SUB, width:] = (
            jnp.where(lane < LANES // 2, jnp.full((SUB, LANES), right, f32), jnp.full((SUB, LANES), left, f32))
            * (tau_step * fidelity)
        )
    one = jnp.ones((SUB, LANES), f32)
    last_col = (c == n_cols - 1).astype(f32)
    first_col = (c == 0).astype(f32)
    last_row = (r == n_rows - 1).astype(f32)
    first_row = (r == 0).astype(f32)
    edge_lane = (lane == LANES - 1).astype(f32)
    edge_sub = (sublane == SUB - 1).astype(f32)
    colmask[:, :LANES] = one - edge_lane * last_col
    colmask[:, LANES:] = one - edge_lane * first_col

    def fill_rows(k, _):
        rowmask[pl.ds(k * SUB, SUB), :] = one
        return 0

    lax.fori_loop(0, chunks + 4, fill_rows, 0)
    rowmask[SUB:2 * SUB, :] = one - edge_sub * first_row
    rowmask[TOP + height - SUB:TOP + height, :] = one - edge_sub * last_row
    zero_wide = jnp.zeros((SUB, wide), f32)
    p1[0:SUB, :] = zero_wide
    u[0:SUB, :] = zero_wide
    bottom = slice(TOP + height + SUB, TOP + height + 2 * SUB)
    u[bottom, :] = zero_wide
    v[bottom, :] = zero_wide

    pl.semaphore_wait(barrier, n_rows + n_cols - 2)
    for load in loads:
        load.wait()

    left_cols = slice(0, LANES)
    right_cols = slice(width - LANES, width)
    for side, cols in enumerate((left_cols, right_cols)):
        take = slice(0, SUB) if side == 0 else slice(LANES - SUB, LANES)
        strip_out[side, 0:SUB, :] = lab[:, cols].astype(f32).T[take]
        strip_out[side, SUB:2 * SUB, :] = img[TOP:TOP + height, cols].T[take]
        strip_out[side, 2 * SUB:, :] = edge[TOP:TOP + height, cols].T[take]
    strips = [
        remote(strip_out.at[0], strip_in.at[0], strip_send.at[0], strip_recv.at[0], col_peer(n_cols - 1)),
        remote(strip_out.at[1], strip_in.at[1], strip_send.at[1], strip_recv.at[1], col_peer(1)),
    ]
    for strip in strips:
        strip.start()

    zero = jnp.zeros((SUB, LANES), f32)

    def lane_sum(x):
        total = x[:, :LANES]
        for k in range(1, width // LANES):
            total = total + x[:, k * LANES:(k + 1) * LANES]
        return total

    def add_sums(acc, field, image):
        rest = 1.0 - field
        return (
            acc[0] + lane_sum(field * image),
            acc[1] + lane_sum(field),
            acc[2] + lane_sum(rest * image),
            acc[3] + lane_sum(rest),
        )

    def first(k, acc):
        rows = pl.ds(pl.multiple_of(TOP + k * SUB, SUB), SUB)
        field = lab[pl.ds(pl.multiple_of(k * SUB, SUB), SUB), :].astype(f32)
        u[rows, :width] = field
        return add_sums(acc, field, img[rows, :width])

    acc = lax.fori_loop(0, chunks, first, (zero,) * 4, unroll=4)

    def start_a(it, acc):
        stacked = jnp.concatenate([jnp.sum(x, axis=0, keepdims=True) for x in acc] + [zero[:SUB - 4]], axis=0)
        part_a[it] = stacked
        copies = [
            remote(part_a.at[it], got_a.at[it, d - 1], a_send.at[it, d - 1], a_recv.at[it, d - 1], row_peer(d))
            for d in range(1, n_rows)
        ]
        for copy in copies:
            copy.start()
        return copies

    def start_b(it, copies):
        for copy in copies:
            copy.wait()
        total = part_a[it]
        for d in range(n_rows - 1):
            total = total + got_a[it, d]
        part_b[it] = total
        copies = [
            remote(part_b.at[it], got_b.at[it, d - 1], b_send.at[it, d - 1], b_recv.at[it, d - 1], col_peer(d))
            for d in range(1, n_cols)
        ]
        for copy in copies:
            copy.start()
        return copies

    def means(it, copies):
        for copy in copies:
            copy.wait()
        total = part_b[it]
        for d in range(n_cols - 1):
            total = total + got_b[it, d]
        sums = jnp.sum(total, axis=1, keepdims=True)
        return (sums[0:1] / sums[1:2], sums[2:3] / sums[3:4])

    pending = start_a(0, acc)

    for strip in strips:
        strip.wait()
    middle = jnp.ones((LANES - 2 * SUB, height), f32)
    for k, buf in enumerate((u, img, edge)):
        part = slice(k * SUB, (k + 1) * SUB)
        buf[TOP:TOP + height, width:] = jnp.concatenate(
            [strip_in[0, part, :], middle, strip_in[1, part, :]], axis=0
        ).T
    rims = []
    for k, buf in enumerate((u, img, edge)):
        rims.append(remote(
            buf.at[pl.ds(TOP, SUB)], buf.at[pl.ds(TOP + height, SUB)],
            rim_send.at[2 * k], rim_recv.at[2 * k], row_peer(n_rows - 1)))
        rims.append(remote(
            buf.at[pl.ds(TOP + height - SUB, SUB)], buf.at[pl.ds(TOP - SUB, SUB)],
            rim_send.at[2 * k + 1], rim_recv.at[2 * k + 1], row_peer(1)))
    for rim in rims:
        rim.start()
    for rim in rims:
        rim.wait()

    def band_of(k):
        return (k - 2 + TILE // SUB) // (TILE // SUB)

    def weights(k):
        return wmap[pl.ds(pl.multiple_of(band_of(k) * SUB, SUB), SUB), :]

    wide_sub = lax.broadcasted_iota(jnp.int32, (SUB, wide), 0)

    def rows_at(start, j):
        base = pl.multiple_of(start * SUB, SUB)
        return pl.ds(pl.multiple_of(base + j * SUB, SUB), SUB)

    def dual(it, start, count):
        source = u if it == 0 else v
        fields = [source[rows_at(start, j), :] for j in range(count + 1)]
        cut = width - LANES
        results = []
        for j in range(count):
            rows = rows_at(start, j)
            here = fields[j]
            gx = pltpu.roll(jnp.where(wide_sub == 0, fields[j + 1], here), SUB - 1, 0) - here
            gy = pltpu.roll(here, wide - 1, 1) - here
            if it == 0:
                q1, q2 = gx * sigma_step, gy * sigma_step
            else:
                old1, old2 = p1[rows, :], p2[rows, :]
                q1, q2 = old1 + gx, old2 + gy
            q1 = q1 * jnp.concatenate([rowmask[rows, :]] * (wide // LANES), axis=1)
            q2 = jnp.concatenate([q2[:, :cut], q2[:, cut:] * colmask[...]], axis=1)
            shrink = jnp.minimum(1.0, edge[rows, :] * lax.rsqrt(q1 * q1 + q2 * q2))
            q1, q2 = q1 * shrink, q2 * shrink
            if it >= ITERS_BEFORE:
                live = weights(start + j) > 0.0
                q1, q2 = jnp.where(live, q1, old1), jnp.where(live, q2, old2)
            results.append((q1, q2))
        before = p1[rows_at(start, -1), :]
        ahead = []
        for j, (q1, q2) in enumerate(results):
            shifted = pltpu.roll(jnp.where(wide_sub == SUB - 1, before, q1), 1, 0)
            div = (q1 - shifted) + (q2 - pltpu.roll(q2, 1, 1))
            old = fields[j] if it == 0 else u[rows_at(start, j), :]
            ahead.append(old + div * tau_step)
            before = q1
        for j, (q1, q2) in enumerate(results):
            rows = rows_at(start, j)
            p1[rows, :] = q1
            if it < ITERS - 1:
                p2[rows, :] = q2
            moved[rows, :] = ahead[j]

    def primal(it, start, count, slope, middle_mean):
        results = []
        for j in range(count):
            rows = rows_at(start, j)
            old = u[rows, :]
            image = img[rows, :]
            w = weights(start + j)
            new = jnp.clip(moved[rows, :] - w * (slope * (image - middle_mean)), 0.0, 1.0)
            if it >= ITERS_BEFORE:
                new = jnp.where(w > 0.0, new, old)
            results.append((old, new, image, w))
        return results

    for it in range(ITERS):
        half = chunks // 2 + 2

        def dual_loop(lo, hi):
            whole = (hi - lo) // BATCH

            def step(k, _):
                dual(it, lo + k * BATCH, BATCH)
                return 0
            lax.fori_loop(0, whole, step, 0)
            if lo + whole * BATCH < hi:
                dual(it, lo + whole * BATCH, hi - lo - whole * BATCH)

        dual_loop(1, half)
        pending = start_b(it, pending)
        dual_loop(half, chunks + 3)
        c1, c2 = means(it, pending)
        slope = 2.0 * (c2 - c1)
        middle_mean = 0.5 * (c1 + c2)

        def update(start, count):
            results = primal(it, start, count, slope, middle_mean)
            for j, (old, new, image, w) in enumerate(results):
                ahead = new + (new - old)
                if it == ITERS_BEFORE - 1:
                    ahead = jnp.where(w > 0.0, ahead, new)
                u[rows_at(start, j), :] = new
                v[rows_at(start, j), :] = ahead * sigma_step
            return results

        if it < ITERS - 1:
            update(1, 1)

            def step(k, acc):
                for _, new, image, _ in update(2 + k * BATCH, BATCH):
                    acc = add_sums(acc, new[:, :width], image[:, :width])
                return acc

            acc = lax.fori_loop(0, chunks // BATCH, step, (zero,) * 4)
            pending = start_a(it + 1, acc)
            update(chunks + 2, 1)
        else:
            def last(k, _):
                results = primal(it, 2 + k * BATCH, BATCH, slope, middle_mean)
                per_tile = TILE // SUB // BATCH
                row = k // per_tile
                for j, (_, new, _, _) in enumerate(results):
                    at = pl.ds(pl.multiple_of(lax.rem(k, per_tile) * (BATCH * SUB) + j * SUB, SUB), SUB)
                    for t in range(tiles_across):
                        tiles[row * tiles_across + t, at, :] = new[:, t * TILE:(t + 1) * TILE]
                return 0

            lax.fori_loop(0, chunks // BATCH, last, 0)

    own_owner = [
        owner_ref[r * tiles_down + a, c * tiles_across + b]
        for a in range(tiles_down) for b in range(tiles_across)
    ]
    step_rows = 32

    def fill(dst, k):
        source = jnp.int32(0)
        used = jnp.int32(0)
        for t, o in enumerate(own_owner):
            hit = (o >= k * slots) & (o < (k + 1) * slots)
            source = jnp.where(hit, t, source)
            used = jnp.where(hit, 1, used)
        scale = used.astype(f32)

        def step(j, _):
            at = pl.ds(pl.multiple_of(j * step_rows, step_rows), step_rows)
            dst[at, :] = tiles[source, at, :] * scale
            return 0

        lax.fori_loop(0, TILE // step_rows, step, 0)

    sends = []
    for d in list(range(1, n_rows)):
        fill(pack.at[d - 1], lax.rem(r + d, n_rows))
        copy = remote(pack.at[d - 1], recv.at[r], t_send.at[d - 1], t_recv.at[d - 1], row_peer(d))
        copy.start()
        sends.append(copy)
    fill(recv.at[r], r)

    origin = []
    for s in range(slots):
        def look(a, carry):
            source, used = carry
            for b in range(tiles_across):
                hit = owner_ref[a, c * tiles_across + b] == r * slots + s
                source = jnp.where(hit, a // tiles_down, source)
                used = jnp.where(hit, 1, used)
            return source, used
        origin.append(lax.fori_loop(0, total_bands, look, (jnp.int32(0), jnp.int32(0))))

    for copy in sends:
        copy.wait()
    for s in range(slots):
        source, used = origin[s]
        scale = used.astype(f32)

        def step(j, _):
            at = pl.ds(pl.multiple_of(j * step_rows, step_rows), step_rows)
            out_ref[s, 0, at, :] = recv[source, at, :] * scale
            return 0

        lax.fori_loop(0, TILE // step_rows, step, 0)


def body(n_rows, n_cols, intensity, edge_weight, labels, tile_cost, tile_owner):
    height, width = intensity.shape
    tiles_down, tiles_across = height // TILE, width // TILE
    slots = tiles_down * tiles_across // 2
    f32 = jnp.float32
    full = pltpu.VMEM((TOP + height + TOP, width + LANES), f32)
    dma = pltpu.SemaphoreType.DMA
    anywhere = pl.BlockSpec(memory_space=pl.ANY)
    smem = pl.BlockSpec(memory_space=pltpu.SMEM)
    return pl.pallas_call(
        functools.partial(kernel, n_rows, n_cols),
        out_shape=jax.ShapeDtypeStruct((slots, 1, TILE, TILE), f32),
        in_specs=[smem, smem, anywhere, anywhere, anywhere],
        out_specs=pl.BlockSpec(memory_space=pltpu.VMEM),
        scratch_shapes=[
            full,
            full,
            pltpu.VMEM((height, width), jnp.int32),
            full,
            full,
            full,
            full,
            full,
            pltpu.VMEM(((tiles_down + 2) * SUB, width + LANES), f32),
            pltpu.VMEM((SUB, 2 * LANES), f32),
            pltpu.VMEM((TOP + height + TOP, LANES), f32),
            pltpu.VMEM((2, 3 * SUB, height), f32),
            pltpu.VMEM((2, 3 * SUB, height), f32),
            pltpu.VMEM((ITERS, SUB, LANES), f32),
            pltpu.VMEM((ITERS, n_rows - 1, SUB, LANES), f32),
            pltpu.VMEM((ITERS, SUB, LANES), f32),
            pltpu.VMEM((ITERS, n_cols - 1, SUB, LANES), f32),
            pltpu.VMEM((tiles_down * tiles_across, TILE, TILE), f32),
            pltpu.VMEM((n_rows - 1, TILE, TILE), f32),
            pltpu.VMEM((n_rows, TILE, TILE), f32),
            dma((3,)),
            dma((2,)),
            dma((2,)),
            dma((6,)),
            dma((6,)),
            dma((ITERS, n_rows - 1)),
            dma((ITERS, n_rows - 1)),
            dma((ITERS, n_cols - 1)),
            dma((ITERS, n_cols - 1)),
            dma((n_rows - 1,)),
            dma((n_rows - 1,)),
        ],
        compiler_params=pltpu.CompilerParams(
            collective_id=0, has_side_effects=True, vmem_limit_bytes=56 * 1024 * 1024
        ),
    )(tile_cost, tile_owner, intensity, edge_weight, labels)


def solution(mesh):
    return jax.shard_map(
        functools.partial(body, mesh.shape["rows"], mesh.shape["cols"]),
        mesh=mesh,
        in_specs=(P("rows", "cols"), P("rows", "cols"), P("rows", "cols"), P(), P()),
        out_specs=P("rows", "cols", None, None),
        check_vma=False,
    )
```

profile of v0, /device:TPU:1, one launch (start us, length us, event | category | flops | bytes accessed | tf_op | source)
XLA Modules:
  0.0 74.9 jit_solution(8212007655797335617)
XLA Ops:
  0.0 72.6 %shard_map.55 = f32[4,1,256,256]{3,2,1,0:T(8,128)} custom-call(s32[16,16]{1,0:T(8,128)} %cost_ref.1, s32[16,16]{1,0:T(8,128)} %owner_ref.1, f32[512,1024]{1,0:T(8,128)} %i_hbm.1, f32[512,1024]{1,0:T(8,128)} %e_hbm.1, s32[512,1024]{1,0:T(8,128)} %l_hbm.1), custom_call_target="tpu_custom_call" | custom-call | tf_op jit(solution)/shard_map/pallas_call | solution.py:429
  72.6 2.3 %copy.7 = f32[4,1,256,256]{3,2,1,0:T(8,128)} copy(f32[4,1,256,256]{3,2,1,0:T(8,128)} %shard_map.55) | data formatting | bytes 2097152
where the time goes:
time: 75.2 us; the launch traced here: 74.9 us
  Pallas kernels  72.6 us (97%)
  local copies, waits for them, and re-layouts  2.29 us (3%)
    pallas_call x1, Pallas kernels, body(): pl.pallas_call(functools.partial(kernel, n_rows, n_cols), out_shape=jax.S...  72.6 us
    unnamed x1, local copies, waits for them, and re-layouts  2.29 us

commit v1 on v0

v1 whole, which is shorter than its diff:
```python
import functools

import jax
import jax.numpy as jnp
from jax import lax
from jax.experimental import pallas as pl
from jax.experimental.pallas import tpu as pltpu
from jax.sharding import PartitionSpec as P

TILE = 256
ITERS_BEFORE = 2
ITERS_AFTER = 2
ITERS = ITERS_BEFORE + ITERS_AFTER

sigma_step = 0.35
tau_step = 0.35
fidelity = 1.0

SUB = 8
LANES = 128
TOP = 2 * SUB
PRIMAL_BATCH = 4
HALVES = TILE // LANES


def kernel(
    n_rows,
    n_cols,
    cost_ref,
    owner_ref,
    i_hbm,
    e_hbm,
    l_hbm,
    out_ref,
    lab,
    img,
    edge,
    ua,
    ub,
    v,
    gy,
    p1,
    p2,
    moved,
    wmap,
    smap,
    colmask,
    rowmask,
    strip_out,
    strip_in,
    part,
    got,
    pack,
    recv,
    load_sem,
    strip_send,
    strip_recv,
    rim_send,
    rim_recv,
    a_send,
    a_recv,
    t_send,
    t_recv,
):
    height = strip_out.shape[2]
    blocks = lab.shape[0]
    every = blocks + 1
    width = blocks * LANES
    tiles_down, tiles_across = height // TILE, width // TILE
    slots = out_ref.shape[0]
    r = lax.axis_index("rows")
    c = lax.axis_index("cols")
    chunks = height // SUB
    f32 = jnp.float32
    own = pl.ds(TOP, height)

    def load(k, b):
        src = (l_hbm, i_hbm, e_hbm)[k].at[:, pl.ds(b * LANES, LANES)]
        dst = (lab, img, edge)[k].at[b, own, :]
        return pltpu.make_async_copy(src, dst, load_sem.at[k, b])

    ends = [0, blocks - 1]
    inner = list(range(1, blocks - 1))
    order = [(k, b) for b in ends for k in range(3)]
    order += [(k, b) for b in inner for k in range(2)] + [(2, b) for b in inner]
    for k, b in order:
        load(k, b).start()

    def peer(dr, dc):
        return (lax.rem(r + dr, n_rows), lax.rem(c + dc, n_cols))

    others = [(dr, dc) for dr in range(n_rows) for dc in range(n_cols) if dr or dc]
    barrier = pltpu.get_barrier_semaphore()
    for dr, dc in others:
        pl.semaphore_signal(barrier, inc=1, device_id=peer(dr, dc), device_id_type=pl.DeviceIdType.MESH)

    def remote(src, dst, send, arrived, to):
        return pltpu.make_async_remote_copy(
            src_ref=src, dst_ref=dst, send_sem=send, recv_sem=arrived,
            device_id=to, device_id_type=pl.DeviceIdType.MESH,
        )

    lane = lax.broadcasted_iota(jnp.int32, (SUB, LANES), 1)
    sublane = lax.broadcasted_iota(jnp.int32, (SUB, LANES), 0)
    total_bands = n_rows * tiles_down
    total_across = n_cols * tiles_across
    bands = tiles_down + 2
    for band in range(bands):
        tr = jnp.clip(r * tiles_down + band - 1, 0, total_bands - 1)
        for t in range(tiles_across):
            w = cost_ref[tr, c * tiles_across + t].astype(f32)
            for h in range(HALVES):
                wmap[band, t * HALVES + h] = jnp.full((SUB, LANES), w * (tau_step * fidelity), f32)
        right = cost_ref[tr, jnp.clip((c + 1) * tiles_across, 0, total_across - 1)].astype(f32)
        left = cost_ref[tr, jnp.clip(c * tiles_across - 1, 0, total_across - 1)].astype(f32)
        wmap[band, blocks] = (
            jnp.where(lane < LANES // 2, jnp.full((SUB, LANES), right, f32), jnp.full((SUB, LANES), left, f32))
            * (tau_step * fidelity)
        )
    one = jnp.ones((SUB, LANES), f32)
    zero = jnp.zeros((SUB, LANES), f32)
    last_col = (c == n_cols - 1).astype(f32)
    first_col = (c == 0).astype(f32)
    last_row = (r == n_rows - 1).astype(f32)
    first_row = (r == 0).astype(f32)
    edge_lane = (lane == LANES - 1).astype(f32)
    edge_sub = (sublane == SUB - 1).astype(f32)
    colmask[0] = one - edge_lane * last_col
    colmask[1] = one - edge_lane * first_col

    def fill_rows(k, _):
        rowmask[pl.ds(pl.multiple_of(k * SUB, SUB), SUB), :] = one
        return 0

    lax.fori_loop(0, chunks + 4, fill_rows, 0, unroll=4)
    rowmask[SUB:2 * SUB, :] = one - edge_sub * first_row
    rowmask[TOP + height - SUB:TOP + height, :] = one - edge_sub * last_row
    bottom = slice(TOP + height + SUB, TOP + height + 2 * SUB)
    for b in range(every):
        p1[b, 0:SUB, :] = zero
        v[b, bottom, :] = zero

    for b in ends:
        for k in range(3):
            load(k, b).wait()
    for side, b in enumerate(ends):
        take = slice(0, SUB) if side == 0 else slice(LANES - SUB, LANES)
        strip_out[side, 0:SUB, :] = lab[b, TOP:TOP + height, :].astype(f32).T[take]
        strip_out[side, SUB:2 * SUB, :] = img[b, TOP:TOP + height, :].T[take]
        strip_out[side, 2 * SUB:, :] = edge[b, TOP:TOP + height, :].T[take]
    pl.semaphore_wait(barrier, len(others))
    strips = []
    for side, dc in enumerate((n_cols - 1, 1)):
        out, into = strip_out.at[side], strip_in.at[side]
        pieces = (
            (0, pl.ds(0, height), pl.ds(LANES, height)),
            (n_rows - 1, pl.ds(0, LANES), pl.ds(LANES + height, LANES)),
            (1, pl.ds(height - LANES, LANES), pl.ds(0, LANES)),
        )
        for k, (dr, mine, theirs) in enumerate(pieces):
            strips.append(remote(
                out.at[:, mine], into.at[:, theirs],
                strip_send.at[side, k], strip_recv.at[side, k], peer(dr, dc)))
    for strip in strips:
        strip.start()

    def add_sums(acc, fields, images):
        su, si, st = fields[0], images[0], fields[0] * images[0]
        for field, image in zip(fields[1:], images[1:]):
            su, si, st = su + field, si + image, st + field * image
        count = float(len(fields))
        return (acc[0] + st, acc[1] + su, acc[2] + (si - st), acc[3] + (count - su))

    acc = (zero,) * 4
    for b in ends + inner:
        if b in inner:
            load(0, b).wait()
            load(1, b).wait()

        def first(k, acc, b=b):
            base = pl.multiple_of(TOP + k * (PRIMAL_BATCH * SUB), SUB)
            fields, images = [], []
            for j in range(PRIMAL_BATCH):
                rows = pl.ds(pl.multiple_of(base + j * SUB, SUB), SUB)
                field = lab[b, rows, :].astype(f32)
                ua[b, rows, :] = field
                fields.append(field)
                images.append(img[b, rows, :])
            return add_sums(acc, fields, images)

        acc = lax.fori_loop(0, chunks // PRIMAL_BATCH, first, acc, unroll=2)

    def start_sums(it, acc):
        stacked = jnp.concatenate([jnp.sum(x, axis=0, keepdims=True) for x in acc] + [zero[:SUB - 4]], axis=0)
        total = jnp.sum(stacked, axis=1, keepdims=True)
        row = jnp.sum(jnp.where(sublane == lane, total, 0.0), axis=0, keepdims=True)
        part[it] = row
        got[it, len(others):, :] = row
        copies = [
            remote(part.at[it], got.at[it, pl.ds(i, 1)], a_send.at[it, i], a_recv.at[it, i], peer(dr, dc))
            for i, (dr, dc) in enumerate(others)
        ]
        for copy in copies:
            copy.start()
        return copies

    def means(it, copies):
        for copy in copies:
            copy.wait_recv()
        total = jnp.sum(got[it], axis=0, keepdims=True)
        sums = [jnp.broadcast_to(total[:, k:k + 1], (SUB, LANES)) for k in range(4)]
        for copy in copies:
            copy.wait_send()
        return sums[0] / sums[1], sums[2] / sums[3]

    pending = start_sums(0, acc)

    for b in inner:
        load(2, b).wait()
    rims = []
    for k, buf in enumerate((lab, img, edge)):
        part_of = pl.ds(0, blocks)
        rims.append(remote(
            buf.at[part_of, pl.ds(TOP, SUB)], buf.at[part_of, pl.ds(TOP + height, SUB)],
            rim_send.at[2 * k], rim_recv.at[2 * k], peer(n_rows - 1, 0)))
        rims.append(remote(
            buf.at[part_of, pl.ds(TOP + height - SUB, SUB)], buf.at[part_of, pl.ds(TOP - SUB, SUB)],
            rim_send.at[2 * k + 1], rim_recv.at[2 * k + 1], peer(1, 0)))
    for rim in rims:
        rim.start()

    for strip in strips:
        strip.wait()
    middle = jnp.ones((LANES - 2 * SUB, height + 2 * LANES), f32)
    for k, buf in enumerate((ua, img, edge)):
        rows_of = slice(k * SUB, (k + 1) * SUB)
        block = jnp.concatenate([strip_in[0, rows_of, :], middle, strip_in[1, rows_of, :]], axis=0).T
        buf[blocks, TOP - SUB:TOP + height + SUB, :] = block[LANES - SUB:LANES + height + SUB]
    for rim in rims:
        rim.wait()
    for b in range(blocks):
        for rows in (slice(TOP - SUB, TOP), slice(TOP + height, TOP + height + SUB)):
            ua[b, rows, :] = lab[b, rows, :].astype(f32)

    groups = chunks + 2
    batch = next(n for n in (6, 3, 2, 1) if groups % n == 0)
    steps = groups // batch
    per_band = TILE // SUB

    def band_of(g):
        return (g - 2 + per_band) // per_band

    def rows_of_group(g, shift=0):
        base = pl.multiple_of(g * SUB, SUB)
        return pl.ds(base + shift if shift else base, SUB)

    at_last = lane == LANES - 1
    at_first = lane == 0

    def live_of(g):
        return [wmap[band_of(g), b] > 0.0 for b in range(every)]

    def stage_grad(it, new_u, old_u, s):
        for j in range(batch):
            g = 1 + s * batch + j
            rows = rows_of_group(g)
            live = live_of(g) if it == ITERS_BEFORE else None
            fields = []
            for b in range(every):
                field = new_u[b, rows, :]
                if it > 0:
                    ahead = field + (field - old_u[b, rows, :])
                    field = jnp.where(live[b], ahead, field) if live else ahead
                field = field * sigma_step
                v[b, rows, :] = field
                fields.append(field)
            turned = [pltpu.roll(x, LANES - 1, 1) for x in fields]
            for b in range(every):
                grad = jnp.where(at_last, turned[(b + 1) % every], turned[b]) - fields[b]
                if b == blocks - 1:
                    grad = grad * colmask[0]
                if b == blocks:
                    grad = grad * colmask[1]
                gy[b, rows, :] = grad

    def stage_flux(it, s):
        for j in range(batch):
            g = 1 + s * batch + j
            rows = rows_of_group(g)
            mask = rowmask[rows, :]
            live = live_of(g) if it >= ITERS_BEFORE else None
            for b in range(every):
                q1 = (v[b, rows_of_group(g, 1), :] - v[b, rows, :]) * mask
                q2 = gy[b, rows, :]
                if it > 0:
                    old1, old2 = p1[b, rows, :], p2[b, rows, :]
                    q1, q2 = old1 + q1, old2 + q2
                shrink = jnp.minimum(1.0, edge[b, rows, :] * lax.rsqrt(q1 * q1 + q2 * q2))
                q1, q2 = q1 * shrink, q2 * shrink
                if live:
                    q1, q2 = jnp.where(live[b], q1, old1), jnp.where(live[b], q2, old2)
                p1[b, rows, :] = q1
                p2[b, rows, :] = q2

    def stage_div(it, new_u, s):
        for j in range(batch):
            g = 1 + s * batch + j
            rows = rows_of_group(g)
            live = live_of(g) if it >= ITERS_BEFORE else None
            flux = [p2[b, rows, :] for b in range(every)]
            turned = [pltpu.roll(x, 1, 1) for x in flux]
            for b in range(every):
                left = jnp.where(at_first, turned[(b + every - 1) % every], turned[b])
                div = (p1[b, rows, :] - p1[b, rows_of_group(g, -1), :]) + (flux[b] - left)
                old = new_u[b, rows, :]
                ahead = old + div * tau_step
                moved[b, rows, :] = jnp.where(live[b], ahead, old) if live else ahead

    def dual(it, new_u, old_u):
        stage_grad(it, new_u, old_u, 0)
        if steps > 1:
            stage_grad(it, new_u, old_u, 1)

        def step(s, _):
            stage_div(it, new_u, s - 1 + (steps - s) // steps)
            stage_flux(it, s)
            stage_grad(it, new_u, old_u, s + 2 - ((s + 2) // steps) * (s + 3 - steps))
            return 0

        lax.fori_loop(0, steps, step, 0)
        stage_div(it, new_u, steps - 1)

    def settle(moved_at, image, w, middle_mean):
        return jnp.clip(moved_at - w * (image - middle_mean), 0.0, 1.0)

    fields = (ua, ub)
    for it in range(ITERS):
        new_u, old_u = fields[it % 2], fields[(it + 1) % 2]
        dual(it, new_u, old_u)
        c1, c2 = means(it, pending)
        slope = 2.0 * (c2 - c1)
        middle_mean = 0.5 * (c1 + c2)
        if it == ITERS - 1:
            break
        for band in range(bands):
            for b in range(every):
                smap[band, b] = wmap[band, b] * slope

        def update(g, b, w):
            rows = rows_of_group(g)
            image = img[b, rows, :]
            new = settle(moved[b, rows, :], image, w, middle_mean)
            old_u[b, rows, :] = new
            return new, image

        for g in (1, chunks + 2):
            for b in range(every):
                update(g, b, smap[band_of(g), b])

        def step(k, acc):
            g = 2 + k * PRIMAL_BATCH
            band = band_of(g)
            for b in range(every):
                w = smap[band, b]
                pairs = [update(g + j, b, w) for j in range(PRIMAL_BATCH)]
                if b < blocks:
                    acc = add_sums(acc, [x for x, _ in pairs], [y for _, y in pairs])
            return acc

        acc = lax.fori_loop(0, chunks // PRIMAL_BATCH, step, (zero,) * 4)
        pending = start_sums(it + 1, acc)

    own_owner, own_cost = [], []
    for a in range(tiles_down):
        for b in range(tiles_across):
            own_owner.append(owner_ref[r * tiles_down + a, c * tiles_across + b])
            own_cost.append(cost_ref[r * tiles_down + a, c * tiles_across + b])
    step_rows = 4 * SUB

    def fill(dst, k):
        down, across, cost, used = jnp.int32(0), jnp.int32(0), jnp.int32(0), jnp.int32(0)
        for t, o in enumerate(own_owner):
            hit = (o >= k * slots) & (o < (k + 1) * slots)
            down = jnp.where(hit, t // tiles_across, down)
            across = jnp.where(hit, t % tiles_across, across)
            cost = jnp.where(hit, own_cost[t], cost)
            used = jnp.where(hit, 1, used)
        w = slope * (cost.astype(f32) * (tau_step * fidelity))
        scale = used.astype(f32)
        at_down = [jnp.full((SUB, LANES), down, jnp.int32) == a for a in range(tiles_down)]

        def step(j, _):
            for i in range(step_rows // SUB):
                at = pl.multiple_of(j * step_rows + i * SUB, SUB)
                for h in range(HALVES):
                    b = across * HALVES + h
                    ahead, image = zero, zero
                    for a in range(tiles_down):
                        rows = pl.ds(pl.multiple_of(at + (TOP + a * TILE), SUB), SUB)
                        ahead = jnp.where(at_down[a], moved[b, rows, :], ahead)
                        image = jnp.where(at_down[a], img[b, rows, :], image)
                    dst[h, pl.ds(at, SUB), :] = settle(ahead, image, w, middle_mean) * scale
            return 0

        lax.fori_loop(0, TILE // step_rows, step, 0)

    sends = []
    for d in range(1, n_rows):
        to = peer(d, 0)
        fill(pack.at[d - 1], to[0])
        copy = remote(pack.at[d - 1], recv.at[r], t_send.at[d - 1], t_recv.at[d - 1], to)
        copy.start()
        sends.append(copy)
    fill(recv.at[r], r)

    origin = []
    for s in range(slots):
        def look(a, carry):
            source, used = carry
            for b in range(tiles_across):
                hit = owner_ref[a, c * tiles_across + b] == r * slots + s
                source = jnp.where(hit, a // tiles_down, source)
                used = jnp.where(hit, 1, used)
            return source, used
        origin.append(lax.fori_loop(0, total_bands, look, (jnp.int32(0), jnp.int32(0))))

    for copy in sends:
        copy.wait()
    for s in range(slots):
        source, used = origin[s]
        scale = used.astype(f32)

        def step(j, _):
            at = pl.ds(pl.multiple_of(j * step_rows, step_rows), step_rows)
            for h in range(HALVES):
                out_ref[s, 0, at, h * LANES:(h + 1) * LANES] = recv[source, h, at, :] * scale
            return 0

        lax.fori_loop(0, TILE // step_rows, step, 0)


def body(n_rows, n_cols, intensity, edge_weight, labels, tile_cost, tile_owner):
    height, width = intensity.shape
    blocks = width // LANES
    tiles_down, tiles_across = height // TILE, width // TILE
    slots = tiles_down * tiles_across // 2
    others = n_rows * n_cols - 1
    f32 = jnp.float32
    full = pltpu.VMEM((blocks + 1, TOP + height + TOP, LANES), f32)
    dma = pltpu.SemaphoreType.DMA
    anywhere = pl.BlockSpec(memory_space=pl.ANY)
    smem = pl.BlockSpec(memory_space=pltpu.SMEM)
    return pl.pallas_call(
        functools.partial(kernel, n_rows, n_cols),
        out_shape=jax.ShapeDtypeStruct((slots, 1, TILE, TILE), f32),
        in_specs=[smem, smem, anywhere, anywhere, anywhere],
        out_specs=pl.BlockSpec(memory_space=pltpu.VMEM),
        scratch_shapes=[
            pltpu.VMEM((blocks, TOP + height + TOP, LANES), jnp.int32),
            full,
            full,
            full,
            full,
            full,
            full,
            full,
            full,
            full,
            pltpu.VMEM((tiles_down + 2, blocks + 1, SUB, LANES), f32),
            pltpu.VMEM((tiles_down + 2, blocks + 1, SUB, LANES), f32),
            pltpu.VMEM((2, SUB, LANES), f32),
            pltpu.VMEM((TOP + height + TOP, LANES), f32),
            pltpu.VMEM((2, 3 * SUB, height), f32),
            pltpu.VMEM((2, 3 * SUB, height + 2 * LANES), f32),
            pltpu.VMEM((ITERS, 1, LANES), f32),
            pltpu.VMEM((ITERS, others + 1, LANES), f32),
            pltpu.VMEM((n_rows - 1, HALVES, TILE, LANES), f32),
            pltpu.VMEM((n_rows, HALVES, TILE, LANES), f32),
            dma((3, blocks)),
            dma((2, 3)),
            dma((2, 3)),
            dma((6,)),
            dma((6,)),
            dma((ITERS, others)),
            dma((ITERS, others)),
            dma((n_rows - 1,)),
            dma((n_rows - 1,)),
        ],
        compiler_params=pltpu.CompilerParams(
            collective_id=0, has_side_effects=True, vmem_limit_bytes=58 * 1024 * 1024
        ),
    )(tile_cost, tile_owner, intensity, edge_weight, labels)


def solution(mesh):
    return jax.shard_map(
        functools.partial(body, mesh.shape["rows"], mesh.shape["cols"]),
        mesh=mesh,
        in_specs=(P("rows", "cols"), P("rows", "cols"), P("rows", "cols"), P(), P()),
        out_specs=P("rows", "cols", None, None),
        check_vma=False,
    )
```

time: 75.2 us -> 66.4 us (0.88)
  Pallas kernels: 72.6 us -> 63.8 us
    pallas_call x1, Pallas kernels: 72.6 us -> 63.8 us  [body(): pl.pallas_call(functools.partial(kernel, n_rows, n_cols), out_shape=jax.S...]
where the time goes in v1:
time: 66.4 us; the launch traced here: 66.1 us
  Pallas kernels  63.8 us (96%)
  local copies, waits for them, and re-layouts  2.29 us (3%)
    pallas_call x1, Pallas kernels, body(): pl.pallas_call(functools.partial(kernel, n_rows, n_cols), out_shape=jax.S...  63.8 us
    unnamed x1, local copies, waits for them, and re-layouts  2.29 us

profile of v1, /device:TPU:1, one launch (start us, length us, event | category | flops | bytes accessed | tf_op | source)
XLA Modules:
  0.0 66.1 jit_solution(4408966619548226348)
XLA Ops:
  0.0 63.8 %shard_map.55 = f32[4,1,256,256]{3,2,1,0:T(8,128)} custom-call(s32[16,16]{1,0:T(8,128)} %cost_ref.1, s32[16,16]{1,0:T(8,128)} %owner_ref.1, f32[512,1024]{1,0:T(8,128)} %i_hbm.1, f32[512,1024]{1,0:T(8,128)} %e_hbm.1, s32[512,1024]{1,0:T(8,128)} %l_hbm.1), custom_call_target="tpu_custom_call" | custom-call | tf_op jit(solution)/shard_map/pallas_call | solution.py:453
  63.8 2.3 %copy.7 = f32[4,1,256,256]{3,2,1,0:T(8,128)} copy(f32[4,1,256,256]{3,2,1,0:T(8,128)} %shard_map.55) | data formatting | bytes 2097152

commit v2 on v1

--- a/solution.py
+++ b/solution.py
@@ -90,6 +90,7 @@
         return (lax.rem(r + dr, n_rows), lax.rem(c + dc, n_cols))
 
     others = [(dr, dc) for dr in range(n_rows) for dc in range(n_cols) if dr or dc]
+    others.sort(key=lambda at: (-min(at[1], n_cols - at[1]), -min(at[0], n_rows - at[0])))
     barrier = pltpu.get_barrier_semaphore()
     for dr, dc in others:
         pl.semaphore_signal(barrier, inc=1, device_id=peer(dr, dc), device_id_type=pl.DeviceIdType.MESH)
@@ -190,6 +191,8 @@
 
         acc = lax.fori_loop(0, chunks // PRIMAL_BATCH, first, acc, unroll=2)
 
+    summed = []
+
     def start_sums(it, acc):
         stacked = jnp.concatenate([jnp.sum(x, axis=0, keepdims=True) for x in acc] + [zero[:SUB - 4]], axis=0)
         total = jnp.sum(stacked, axis=1, keepdims=True)
@@ -202,6 +205,7 @@
         ]
         for copy in copies:
             copy.start()
+        summed.extend(copies)
         return copies
 
     def means(it, copies):
@@ -209,8 +213,6 @@
             copy.wait_recv()
         total = jnp.sum(got[it], axis=0, keepdims=True)
         sums = [jnp.broadcast_to(total[:, k:k + 1], (SUB, LANES)) for k in range(4)]
-        for copy in copies:
-            copy.wait_send()
         return sums[0] / sums[1], sums[2] / sums[3]
 
     pending = start_sums(0, acc)
@@ -424,6 +426,8 @@
             return source, used
         origin.append(lax.fori_loop(0, total_bands, look, (jnp.int32(0), jnp.int32(0))))
 
+    for copy in summed:
+        copy.wait_send()
     for copy in sends:
         copy.wait()
     for s in range(slots):

time: 66.4 us -> 66.2 us (level)
  no operation moved by 1% of the time
where the time goes in v2:
time: 66.2 us; the launch traced here: 65.9 us
  Pallas kernels  63.6 us (96%)
  local copies, waits for them, and re-layouts  2.29 us (3%)
    pallas_call x1, Pallas kernels, body(): pl.pallas_call(functools.partial(kernel, n_rows, n_cols), out_shape=jax.S...  63.6 us
    unnamed x1, local copies, waits for them, and re-layouts  2.29 us

profile of v2, /device:TPU:1, one launch (start us, length us, event | category | flops | bytes accessed | tf_op | source)
XLA Modules:
  0.0 65.9 jit_solution(3846634965196693007)
XLA Ops:
  0.0 63.6 %shard_map.55 = f32[4,1,256,256]{3,2,1,0:T(8,128)} custom-call(s32[16,16]{1,0:T(8,128)} %cost_ref.1, s32[16,16]{1,0:T(8,128)} %owner_ref.1, f32[512,1024]{1,0:T(8,128)} %i_hbm.1, f32[512,1024]{1,0:T(8,128)} %e_hbm.1, s32[512,1024]{1,0:T(8,128)} %l_hbm.1), custom_call_target="tpu_custom_call" | custom-call | tf_op jit(solution)/shard_map/pallas_call | solution.py:457
  63.6 2.3 %copy.7 = f32[4,1,256,256]{3,2,1,0:T(8,128)} copy(f32[4,1,256,256]{3,2,1,0:T(8,128)} %shard_map.55) | data formatting | bytes 2097152
